TPU v7x, 32 devices: a whole 2x2x4 slice. The times are simulated.
32 devices in a mesh: dp: 8 (over z, x), head: 4 (over y, core).
Axes of the slice: x: 2, y: 2, z: 4, core: 2. Of those that a mesh axis runs over, the one named last changes fastest.
Arguments:
- tokens: bfloat16 [11840, 768], P(('dp', 'head')), may hold values from -6 to 6
- caption_len: int32 [64], P('dp'), may hold values from 5 to 40, as said below
- first_gain: bfloat16 [768], P(('dp', 'head')), may hold values from 0.5 to 1.5
- first_shift: bfloat16 [768], P(('dp', 'head')), may hold values from -3 to 3
- qkv_weight: bfloat16 [768, 3, 768], P('dp', None, 'head'), may hold values from -0.21875 to 0.21875
- qkv_bias: bfloat16 [2, 768], P(None, ('head', 'dp')), may hold values from -3 to 3
- out_weight: bfloat16 [768, 768], P(('dp', 'head')), may hold values from -1.25 to 1.25
- out_bias: bfloat16 [768], P(('dp', 'head')), may hold values from -3 to 3
- second_gain: bfloat16 [768], P(('dp', 'head')), may hold values from 0.5 to 1.5
- second_shift: bfloat16 [768], P(('dp', 'head')), may hold values from -3 to 3
- up_weight: bfloat16 [768, 3072], P('dp', 'head'), may hold values from -0.21875 to 0.21875
- up_bias: bfloat16 [3072], P(('head', 'dp')), may hold values from -3 to 3
- down_weight: bfloat16 [3072, 768], P('head', 'dp'), may hold values from -0.109375 to 0.109375
- down_bias: bfloat16 [768], P(('dp', 'head')), may hold values from -3 to 3
- output_grad: bfloat16 [11840, 768], P(('dp', 'head')), may hold values from -6 to 6
Outputs:
- layer_out: bfloat16 [11840, 768], P(('dp', 'head'))
- tokens_grad: bfloat16 [11840, 768], P(('dp', 'head'))
- first_gain_grad: float32 [768], P(('dp', 'head'))
- first_shift_grad: float32 [768], P(('dp', 'head'))
- qkv_weight_grad: float32 [768, 3, 768], P('dp', None, 'head')
- qkv_bias_grad: float32 [2, 768], P(None, ('head', 'dp'))
- out_weight_grad: float32 [768, 768], P(('dp', 'head'))
- out_bias_grad: float32 [768], P(('dp', 'head'))
- second_gain_grad: float32 [768], P(('dp', 'head'))
- second_shift_grad: float32 [768], P(('dp', 'head'))
- up_weight_grad: float32 [768, 3072], P('dp', 'head')
- up_bias_grad: float32 [3072], P(('head', 'dp'))
- down_weight_grad: float32 [3072, 768], P('head', 'dp')
- down_bias_grad: float32 [768], P(('dp', 'head'))
Inputs may be any that keep to these rules, and one draw needn't show every extreme that they name: Each pair's caption fills its first caption_len slots; some pair's caption fills all 40 slots.
All inputs are finite; a program needn't handle non-finite values.
Results may differ from a plain program's by a relative error of at most 0.014.
Values may be sent and summed in bfloat16 or wider, within the bound.
No kernel may reach another device: no remote copies, remote signals or barrier semaphores. Data moves between devices by JAX's collectives and lax.ppermute only.
A program may use at most 128 MiB of HBM per device.

v0:
```python
from functools import partial
import jax
import jax.numpy as jnp
from jax import lax
from jax.sharding import PartitionSpec as P

HEAD_DIM = 64
TEXT = 40


def norm_rows(values, gain, shift):
    centre = jnp.mean(values, axis=-1, keepdims=True)
    spread = values - centre
    second = jnp.mean(spread * spread, axis=-1, keepdims=True)
    return spread * lax.rsqrt(second + 1e-06) * gain + shift


def contract_rows(former, latter):
    return lax.dot_general(
        former, latter, (((0,), (0,)), ((), ())), preferred_element_type=jnp.float32
    )


def times_transposed(former, latter):
    return lax.dot_general(
        former, latter, (((1,), (1,)), ((), ())), preferred_element_type=jnp.float32
    )


def column_sum(matrix):
    return jnp.sum(matrix.astype(jnp.float32), axis=0)


def local(
    tokens,
    caption_len,
    first_gain,
    first_shift,
    qkv_weight,
    qkv_bias,
    out_weight,
    out_bias,
    second_gain,
    second_shift,
    up_weight,
    up_bias,
    down_weight,
    down_bias,
    output_grad,
):
    width = tokens.shape[1]
    gain_one, shift_one, w_out, b_out, gain_two, shift_two, b_down = (
        lax.all_gather(first_gain, ("dp", "head"), axis=0, tiled=True),
        lax.all_gather(first_shift, ("dp", "head"), axis=0, tiled=True),
        lax.all_gather(out_weight, ("dp", "head"), axis=0, tiled=True),
        lax.all_gather(out_bias, ("dp", "head"), axis=0, tiled=True),
        lax.all_gather(second_gain, ("dp", "head"), axis=0, tiled=True),
        lax.all_gather(second_shift, ("dp", "head"), axis=0, tiled=True),
        lax.all_gather(down_bias, ("dp", "head"), axis=0, tiled=True),
    )
    w_qkv, b_qkv, w_up, b_up, w_down = (
        lax.all_gather(qkv_weight, "dp", axis=0, tiled=True),
        lax.all_gather(qkv_bias, "dp", axis=1, tiled=True),
        lax.all_gather(up_weight, "dp", axis=0, tiled=True),
        lax.all_gather(up_bias, "dp", axis=0, tiled=True),
        lax.all_gather(down_weight, "dp", axis=1, tiled=True),
    )
    local_width = w_qkv.shape[2]
    heads_local = local_width // HEAD_DIM
    flat_qkv = w_qkv.reshape(width, 3 * local_width)
    tok_rows = tokens.astype(jnp.float32)
    normed, first_pull = jax.vjp(
        norm_rows, tok_rows, gain_one.astype(jnp.float32), shift_one.astype(jnp.float32)
    )
    normed_low = normed.astype(jnp.bfloat16)
    whole = lax.all_gather(normed_low, "head", axis=0, tiled=True)
    group_rows = whole.shape[0]
    item_count = caption_len.shape[0]
    seq_length = group_rows // item_count
    projected = jnp.dot(whole, flat_qkv, preferred_element_type=jnp.float32).reshape(
        group_rows, 3, local_width
    )
    bias_rows = jnp.stack([b_qkv[0], jnp.zeros_like(b_qkv[0]), b_qkv[1]]).astype(jnp.float32)
    packed = (
        (projected + bias_rows)
        .astype(jnp.bfloat16)
        .reshape(item_count, seq_length, 3, heads_local, HEAD_DIM)
    )
    queries = packed[:, :, 0]
    key_rows = packed[:, :, 1]
    value_rows = packed[:, :, 2]
    score_scale = HEAD_DIM ** (-0.5)
    position = jnp.arange(seq_length, dtype=jnp.int32)
    visible = ((position[None, :] >= TEXT) | (position[None, :] < caption_len[:, None]))[
        :, None, None, :
    ]

    def masked_scores():
        product = (
            jnp.einsum("ishd,ithd->ihst", queries, key_rows, preferred_element_type=jnp.float32)
            * score_scale
        )
        return jnp.where(visible, product, -1000000000.0)

    scores = masked_scores()
    highest_score = jnp.max(scores, axis=-1, keepdims=True)
    unnormed = jnp.exp(scores - highest_score)
    row_totals = jnp.sum(unnormed, axis=-1, keepdims=True)
    attn_probs = unnormed / row_totals
    log_total = highest_score + jnp.log(row_totals)
    probs_low = attn_probs.astype(jnp.bfloat16)
    context = jnp.einsum(
        "ihst,ithd->ishd", probs_low, value_rows, preferred_element_type=jnp.float32
    )
    context_low = context.astype(jnp.bfloat16).reshape(group_rows, local_width)
    ctx_rows = lax.all_to_all(context_low, "head", split_axis=0, concat_axis=1, tiled=True)
    middle = tok_rows + (
        jnp.dot(ctx_rows, w_out, preferred_element_type=jnp.float32) + b_out.astype(jnp.float32)
    )
    hidden_in, second_pull = jax.vjp(
        norm_rows, middle, gain_two.astype(jnp.float32), shift_two.astype(jnp.float32)
    )
    hidden_low = hidden_in.astype(jnp.bfloat16)
    hidden_group = lax.all_gather(hidden_low, "head", axis=0, tiled=True)
    up_proj = jnp.dot(hidden_group, w_up, preferred_element_type=jnp.float32) + b_up.astype(
        jnp.float32
    )
    active, gelu_pull = jax.vjp(partial(jax.nn.gelu, approximate=False), up_proj)
    active_low = active.astype(jnp.bfloat16)
    branch_part = jnp.dot(active_low, w_down, preferred_element_type=jnp.float32)
    branch = lax.psum_scatter(
        branch_part.astype(jnp.bfloat16), "head", scatter_dimension=0, tiled=True
    ).astype(jnp.float32)
    layer_out = (middle + (branch + b_down.astype(jnp.float32))).astype(jnp.bfloat16)
    w_out = lax.all_gather(out_weight, ("dp", "head"), axis=0, tiled=True)
    w_qkv, w_up, w_down = (
        lax.all_gather(qkv_weight, "dp", axis=0, tiled=True),
        lax.all_gather(up_weight, "dp", axis=0, tiled=True),
        lax.all_gather(down_weight, "dp", axis=1, tiled=True),
    )
    flat_qkv = w_qkv.reshape(width, 3 * local_width)
    grad_top = output_grad.astype(jnp.float32)
    grad_low = grad_top.astype(jnp.bfloat16)
    down_bias_part = column_sum(grad_low)
    grad_group = lax.all_gather(grad_low, "head", axis=0, tiled=True)
    down_weight_part = contract_rows(active_low, grad_group)
    (grad_up,) = gelu_pull(times_transposed(grad_group, w_down))
    up_low = grad_up.astype(jnp.bfloat16)
    up_bias_part = column_sum(up_low)
    up_weight_part = contract_rows(hidden_group, up_low)
    grad_hidden = lax.psum_scatter(
        times_transposed(up_low, w_up).astype(jnp.bfloat16), "head", scatter_dimension=0, tiled=True
    ).astype(jnp.float32)
    grad_middle_part, gain_two_part, shift_two_part = second_pull(grad_hidden)
    grad_middle = grad_top + grad_middle_part
    middle_low = grad_middle.astype(jnp.bfloat16)
    out_bias_part = column_sum(middle_low)
    out_weight_part = contract_rows(ctx_rows, middle_low)
    grad_ctx = times_transposed(middle_low, w_out).astype(jnp.bfloat16)
    grad_context = lax.all_to_all(
        grad_ctx, "head", split_axis=1, concat_axis=0, tiled=True
    ).reshape(item_count, seq_length, heads_local, HEAD_DIM)
    scores = masked_scores()
    attn_probs = jnp.exp(scores - log_total)
    probs_low = attn_probs.astype(jnp.bfloat16)
    grad_probs = jnp.einsum(
        "ishd,ithd->ihst", grad_context, value_rows, preferred_element_type=jnp.float32
    )
    value_grad = jnp.einsum(
        "ihst,ishd->ithd", probs_low, grad_context, preferred_element_type=jnp.float32
    ).astype(jnp.bfloat16)
    grad_scores = attn_probs * (
        grad_probs - jnp.sum(attn_probs * grad_probs, axis=-1, keepdims=True)
    )
    scores_low = grad_scores.astype(jnp.bfloat16)
    query_grad = (
        jnp.einsum("ihst,ithd->ishd", scores_low, key_rows, preferred_element_type=jnp.float32)
        * score_scale
    ).astype(jnp.bfloat16)
    key_grad = (
        jnp.einsum("ihst,ishd->ithd", scores_low, queries, preferred_element_type=jnp.float32)
        * score_scale
    ).astype(jnp.bfloat16)
    grad_packed = jnp.stack([query_grad, key_grad, value_grad], axis=2).reshape(
        group_rows, 3 * local_width
    )
    qkv_weight_part = contract_rows(whole, grad_packed).reshape(width, 3, local_width)
    qkv_bias_part = jnp.stack(
        [column_sum(grad_packed[:, :local_width]), column_sum(grad_packed[:, 2 * local_width :])]
    )
    own_grads = lax.all_to_all(
        grad_packed.reshape(group_rows, 3, local_width),
        "head",
        split_axis=0,
        concat_axis=2,
        tiled=True,
    )
    all_columns = lax.all_gather(w_qkv, "head", axis=2, tiled=True)
    grad_normed = times_transposed(
        own_grads.reshape(own_grads.shape[0], 3 * width), all_columns.reshape(width, 3 * width)
    )
    grad_rows_part, gain_one_part, shift_one_part = first_pull(grad_normed)
    tokens_grad = (grad_middle + grad_rows_part).astype(jnp.bfloat16)
    layer_sums = (
        lax.psum_scatter(gain_one_part, ("dp", "head"), scatter_dimension=0, tiled=True),
        lax.psum_scatter(shift_one_part, ("dp", "head"), scatter_dimension=0, tiled=True),
        lax.psum_scatter(out_weight_part, ("dp", "head"), scatter_dimension=0, tiled=True),
        lax.psum_scatter(out_bias_part, ("dp", "head"), scatter_dimension=0, tiled=True),
        lax.psum_scatter(gain_two_part, ("dp", "head"), scatter_dimension=0, tiled=True),
        lax.psum_scatter(shift_two_part, ("dp", "head"), scatter_dimension=0, tiled=True),
        lax.psum_scatter(down_bias_part, ("dp", "head"), scatter_dimension=0, tiled=True),
    )
    head_sums = (
        lax.psum_scatter(qkv_weight_part, "dp", scatter_dimension=0, tiled=True),
        lax.psum_scatter(qkv_bias_part, "dp", scatter_dimension=1, tiled=True),
        lax.psum_scatter(up_weight_part, "dp", scatter_dimension=0, tiled=True),
        lax.psum_scatter(up_bias_part, "dp", scatter_dimension=0, tiled=True),
        lax.psum_scatter(down_weight_part, "dp", scatter_dimension=1, tiled=True),
    )
    return (
        layer_out,
        tokens_grad,
        layer_sums[0],
        layer_sums[1],
        head_sums[0],
        head_sums[1],
        layer_sums[2],
        layer_sums[3],
        layer_sums[4],
        layer_sums[5],
        head_sums[2],
        head_sums[3],
        head_sums[4],
        layer_sums[6],
    )


def solution(mesh):
    return jax.shard_map(
        local,
        mesh=mesh,
        in_specs=(
            P(("dp", "head"), None),
            P("dp"),
            P(("dp", "head")),
            P(("dp", "head")),
            P("dp", None, "head"),
            P(None, ("head", "dp")),
            P(("dp", "head"), None),
            P(("dp", "head")),
            P(("dp", "head")),
            P(("dp", "head")),
            P("dp", "head"),
            P(("head", "dp")),
            P("head", "dp"),
            P(("dp", "head")),
            P(("dp", "head"), None),
        ),
        out_specs=(
            P(("dp", "head"), None),
            P(("dp", "head"), None),
            P(("dp", "head")),
            P(("dp", "head")),
            P("dp", None, "head"),
            P(None, ("head", "dp")),
            P(("dp", "head"), None),
            P(("dp", "head")),
            P(("dp", "head")),
            P(("dp", "head")),
            P("dp", "head"),
            P(("head", "dp")),
            P("head", "dp"),
            P(("dp", "head")),
        ),
        check_vma=False,
    )
```

profile of v0, /device:TPU:0, one launch (start us, length us, event | category | flops | bytes accessed | tf_op | source)
XLA Modules:
  0.0 709.9 jit_solution(16283716665516034311)
XLA Ops:
  12.3 42.2 %all-reduce.21 = (bf16[768]{0:T(1024)(128)(2,1)S(1)}, bf16[768]{0:T(1024)(128)(2,1)S(1)}, bf16[768]{0:T(1024)(128)(2,1)S(1)}, bf16[768]{0:T(1024)(128)(2,1)S(1)}...) all-reduce(bf16[768]{0:T(1024)(128)(2,1)S(1)} %dynamic-update-slice, ...), channel_id=1, replica_groups=mesh['dp'=8,'head'=4] {'dp','head'}, use_global_device_ids=true, to_apply=%add.1 | all-reduce | flops 4608 | bytes 18432
  54.4 1.2 convert_reduce_fusion.2
  55.7 1.4 fusion.31
  57.0 2.2 fusion.40
  60.7 20.2 %all-gather.1 = bf16[8,24,2]{1,2,0:T(2,128)(2,1)S(1)} all-gather(bf16[1,24,2]{1,2,0:T(2,128)(2,1)S(1)} %bitcast.140), channel_id=1, replica_groups=mesh['dp'=8,'head'=4] {'dp'}, dimensions={0}, use_global_device_ids=true | all-gather | bytes 864 | tf_op jit(solution)/shard_map/all_gather | solution.py:63
  81.2 36.1 %all_gather.55 = bf16[768,3,192]{2,1,0:T(4,128)(2,1)S(1)} all-gather(bf16[96,3,192]{2,1,0:T(4,128)(2,1)S(1)} %copy.56), channel_id=1, replica_groups=mesh['dp'=8,'head'=4] {'dp'}, dimensions={0}, use_global_device_ids=true | all-gather | bytes 995328 | tf_op jit(solution)/shard_map/all_gather | solution.py:62
  118.4 2.3 reshape.228
  120.8 1.4 copy-done.21
  122.2 2.8 add_convert_fusion.1
  125.0 5.0 reshape.198
  130.2 1.7 fusion.53
  132.8 1.3 copy-done
  137.1 3.5 all-to-all-start
  141.2 8.8 %all-to-all-done = bf16[4,370,192]{1,2,0:T(8,128)(2,1)S(1)} async-done(((bf16[4,370,192]{1,2,0:T(8,128)(2,1)}), bf16[4,370,192]{1,2,0:T(8,128)(2,1)S(1)}, u32[]{:S(2)}, u32[]{:S(2)}) %all-to-all-start) | async-done | bytes 568352 | tf_op jit(solution)/shard_map/all_to_all | solution.py:116
  150.1 2.2 fusion.54
  157.2 20.8 %all-reduce.5 = bf16[768]{0:T(1024)(128)(2,1)S(1)} all-reduce(bf16[768]{0:T(1024)(128)(2,1)S(1)} %dynamic-update-slice.5), channel_id=1, replica_groups=mesh['dp'=8,'head'=4] {'dp'}, use_global_device_ids=true, to_apply=%add.5 | all-reduce | flops 768 | bytes 3072
  177.9 3.6 reshape.225
  181.6 9.8 %all-gather.22.cloned.1.call-done = bf16[4,370,768]{2,1,0:T(8,128)(2,1)} async-done(((bf16[1,370,768]{2,1,0:T(8,128)(2,1)}), bf16[4,370,768]{2,1,0:T(8,128)(2,1)}) %all-gather.22.cloned.1.call-update) | async-done | bytes 2273296 | tf_op jit(solution)/shard_map/all_gather | solution.py:124
  191.3 3.7 reshape.223
  195.0 39.5 %all-gather.14.cloned.1.call-done = bf16[768,768]{1,0:T(8,128)(2,1)} async-done(((bf16[96,768]{1,0:T(8,128)(2,1)}), bf16[768,768]{1,0:T(8,128)(2,1)}) %all-gather.14.cloned.1.call-update) | async-done | bytes 1179664 | tf_op jit(solution)/shard_map/all_gather | solution.py:64
  234.5 6.1 fusion.55
  240.6 35.8 %all-gather.16.cloned.1.call-done = bf16[768,768]{0,1:T(8,128)(2,1)} async-done(((bf16[768,96]{0,1:T(8,128)(2,1)}), bf16[768,768]{0,1:T(8,128)(2,1)}) %all-gather.16.cloned.1.call-update) | async-done | bytes 1179664 | tf_op jit(solution)/shard_map/all_gather | solution.py:66
  276.4 14.9 %convert_reduce_fusion = (f32[768]{0:T(1024)}, bf16[1480,768]{1,0:T(8,128)(2,1)S(1)}, f32[1480,768]{1,0:T(8,128)S(1)}) fusion(f32[1480,768]{1,0:T(8,128)} %fusion.55, f32[768]{0:T(1024)S(1)} %convert_element_type.133, bf16[1480,768]{1,0:T(8,128)(2,1)} %reshape.225, bf16[768,768]{0,1:T(8,128)(2,1)} %all-gather.16.cloned.1.call-done), kind=kOutput, calls=%fused_computation.8 | convolution fusion | flops 1831126272 | bytes 14825472 | tf_op jit(solution)/shard_map/dot_general | solution.py:25
  292.2 1.2 copy-done.35
  293.4 3.4 convolution_convert_fusion.1
  296.8 3.5 convolution_convert_fusion
  300.3 54.1 %fusion.46 = (bf16[376,768]{1,0:T(8,128)(2,1)S(1)}, bf16[376,768]{1,0:T(8,128)(2,1)S(1)}) fusion(bf16[1480,768]{1,0:T(8,128)(2,1)} %convolution_convert_fusion.1, bf16[1480,768]{1,0:T(8,128)(2,1)} %convolution_convert_fusion), kind=kCustom, calls=%all-reduce-scatter.2 | all-reduce-scatter fusion | flops 2310145 | bytes 5702144
  354.4 1.3 collective-permute-start
  355.7 3.2 collective-permute-start.1
  360.8 4.2 concatenate.5
  365.1 1.3 concatenate.6
  366.4 1.1 fusion.33
  368.3 3.0 fusion.49
  374.0 3.5 all-to-all-start.1
  377.6 3.5 fusion.57
  381.1 5.9 all-to-all-done.1
  387.0 1.3 copy.66
  388.3 2.5 reshape.199
  390.8 4.4 multiply_reduce_fusion
  395.2 1.1 multiply_convert_fusion
  400.7 2.9 copy.78
  403.6 4.9 reshape.202
  408.5 5.7 fusion.56
  414.5 5.9 fusion.58
  420.4 5.9 fusion.59
  427.5 1.3 copy.69
  428.8 2.7 stack.33
  431.5 2.5 copy.71
  434.0 2.6 stack.34
  436.7 1.4 copy.74
  438.0 2.0 stack.35
  440.0 2.7 pad_maximum_fusion.1
  442.7 5.5 copy.75
  448.2 4.8 all-to-all-start.2
  454.3 1.5 convert_reduce_fusion.5
  455.8 19.6 %all-reduce.20 = (f32[2,192]{1,0:T(2,128)S(1)}, f32[768]{0:T(1024)S(1)}) all-reduce(f32[2,192]{1,0:T(2,128)S(1)} %pad_maximum_fusion.2, f32[768]{0:T(1024)S(1)} %copy-done.28), channel_id=7, replica_groups=mesh['dp'=8,'head'=4] {'dp'}, use_global_device_ids=true, to_apply=%region_20.21.clone | all-reduce | flops 1152 | bytes 9216
  476.6 12.6 %all-to-all-done.2 = bf16[1480,3,192]{2,1,0:T(4,128)(2,1)} async-done(((bf16[1480,3,192]{2,1,0:T(4,128)(2,1)}), bf16[1480,3,192]{2,1,0:T(4,128)(2,1)}, u32[]{:S(2)}, u32[]{:S(2)}) %all-to-all-start.2) | async-done | bytes 1704992 | tf_op jit(solution)/shard_map/all_to_all | solution.py:191
  489.2 5.5 copy.76
  494.7 4.3 fusion.45
  499.7 1.4 convert_reduce_fusion.3
  501.1 39.7 %all-reduce.19 = (f32[768]{0:T(1024)S(1)}, f32[768]{0:T(1024)S(1)}, f32[768]{0:T(1024)S(1)}, f32[768]{0:T(1024)S(1)}, f32[768]{0:T(1024)S(1)}, /*index=5*/f32[768]{0:T(1024)S(1)}) all-reduce(f32[768]{0:T(1024)S(1)} %get-tuple-element.18, f32[768]{0:T(1024)S(1)} %get-tuple-element.20, ...), channel_id=4, replica_groups=mesh['dp'=8,'head'=4] {'dp','head'}, use_global_device_ids=true, to_apply=%region_14.15.clone | all-reduce | flops 4608 | bytes 36864
  544.3 12.9 %reduce-scatter.10.cloned.1.call-done = f32[96,3,192]{2,0,1:T(8,128)} async-done(((f32[768,3,192]{2,0,1:T(8,128)}), f32[96,3,192]{2,0,1:T(8,128)}) %reduce-scatter.10.cloned.1.call-update) | async-done | bytes 221200 | tf_op jit(solution)/shard_map/reduce_scatter | solution.py:214
  557.2 72.8 %reduce-scatter.14.cloned.1.call-done = f32[96,768]{1,0:T(8,128)} async-done(((f32[768,768]{1,0:T(8,128)}), f32[96,768]{1,0:T(8,128)}) %reduce-scatter.14.cloned.1.call-update) | async-done | bytes 294928 | tf_op jit(solution)/shard_map/reduce_scatter | solution.py:216
  630.0 73.0 %reduce-scatter.16.cloned.1.call-done = f32[768,96]{0,1:T(8,128)} async-done(((f32[768,768]{0,1:T(8,128)}), f32[768,96]{0,1:T(8,128)}) %reduce-scatter.16.cloned.1.call-update) | async-done | bytes 294928 | tf_op jit(solution)/shard_map/reduce_scatter | solution.py:218
  (174 shorter events, 33.6 us)
Async XLA Ops:
  7.2 53.5 %copy-start.30 = (bf16[2,24]{1,0:T(2,128)(2,1)S(1)}, bf16[2,24]{1,0:T(2,128)(2,1)}, u32[]{:S(2)}) copy-start(bf16[2,24]{1,0:T(2,128)(2,1)} %param.20) | copy-start | bytes 292
  7.2 73.8 %copy-start.22 = (bf16[96,3,192]{2,0,1:T(8,128)(2,1)S(1)}, bf16[96,3,192]{2,0,1:T(8,128)(2,1)}, u32[]{:S(2)}) copy-start(bf16[96,3,192]{2,0,1:T(8,128)(2,1)} %param.19) | copy-start | bytes 331780
  7.2 111.2 %all-gather.20.cloned.1.call-start = ((), (), s32[]{:S(2)}) async-start(), calls=%async_computation.15 | async-start | bytes 2887680 | tf_op jit(solution)/shard_map/all_gather | solution.py:76
  57.0 61.1 %copy-start.23 = (f32[370]{0:T(512)}, f32[370]{0:T(512)S(1)}, u32[]{:S(2)}) copy-start(f32[370]{0:T(512)S(1)} %fusion.31) | copy-start | bytes 4444
  59.2 82.0 %all-gather.12.cloned.1.call-start = ((), (), s32[]{:S(2)}) async-start(), calls=%async_computation.7 | async-start | bytes 1216512 | tf_op jit(solution)/shard_map/all_gather | solution.py:55
  60.0 118.0 %all-gather.24.cloned.1.call-start = ((), (), s32[]{:S(2)}) async-start(), calls=%async_computation.17 | async-start | bytes 2887680 | tf_op jit(solution)/shard_map/all_gather | solution.py:145
  81.0 37.3 %copy-start.32 = (s32[8]{0:T(128)S(1)}, s32[8]{0:T(128)}, u32[]{:S(2)}) copy-start(s32[8]{0:T(128)} %param.16) | copy-start | bytes 100
  118.2 2.6 copy-start.11
  120.8 1.4 copy-start.21
  130.2 1.7 copy-start.12
  130.2 1.7 copy-start.14
  130.2 2.5 copy-start.16
  131.9 2.1 copy-start
  135.5 14.6 %copy-start.1 = (bf16[370,768]{1,0:T(8,128)(2,1)S(1)}, bf16[370,768]{1,0:T(8,128)(2,1)}, u32[]{:S(2)}) copy-start(bf16[370,768]{1,0:T(8,128)(2,1)} %param.15) | copy-start | bytes 1704964
  137.1 13.0 %all-to-all-start = ((bf16[4,370,192]{1,2,0:T(8,128)(2,1)}), bf16[4,370,192]{1,2,0:T(8,128)(2,1)S(1)}, u32[]{:S(2)}, u32[]{:S(2)}) async-start(bf16[4,370,192]{1,2,0:T(8,128)(2,1)} %copy.64), calls=%async_computation | async-start | bytes 1179648 | tf_op jit(solution)/shard_map/all_to_all | solution.py:116
  140.6 50.7 %all-gather.22.cloned.1.call-start = ((), (), s32[]{:S(2)}) async-start(), calls=%async_computation.16 | async-start | bytes 2887680 | tf_op jit(solution)/shard_map/all_gather | solution.py:124
  150.1 2.5 copy-start.17
  152.3 3.3 copy-start.29
  152.3 4.6 copy-start.36
  152.6 28.9 %copy-start.25 = (f32[370]{0:T(512)}, f32[370]{0:T(512)S(1)}, u32[]{:S(2)}) copy-start(f32[370]{0:T(512)S(1)} %multiply_reduce_fusion.1) | copy-start | bytes 4444
  153.7 80.8 %all-gather.14.cloned.1.call-start = ((), (), s32[]{:S(2)}) async-start(), calls=%async_computation.8 | async-start | bytes 1327104 | tf_op jit(solution)/shard_map/all_gather | solution.py:64
  154.3 122.1 %all-gather.16.cloned.1.call-start = ((), (), s32[]{:S(2)}) async-start(), calls=%async_computation.9 | async-start | bytes 1327104 | tf_op jit(solution)/shard_map/all_gather | solution.py:66
  154.9 339.8 %all-gather.18.cloned.1.call-start = ((), (), s32[]{:S(2)}) async-start(), calls=%async_computation.10 | async-start | bytes 4423680 | tf_op jit(solution)/shard_map/all_gather | solution.py:198
  276.4 14.9 %copy-start.10 = (f32[1480,768]{1,0:T(8,128)S(1)}, f32[1480,768]{1,0:T(8,128)}, u32[]{:S(2)}) copy-start(f32[1480,768]{1,0:T(8,128)} %fusion.55) | copy-start | bytes 13639684
  291.3 5.5 copy-start.20
  291.3 2.1 copy-start.35
  293.4 3.4 copy-start.19
  293.4 3.4 copy-start.34
  300.3 58.7 %copy-start.31 = (u32[32]{0:T(128)S(1)}, u32[32]{0:T(128)}, u32[]{:S(2)}) copy-start(u32[32]{0:T(128)} %constant.130) | copy-start | bytes 388
  354.4 6.4 collective-permute-start
  355.7 9.3 %collective-permute-start.1 = (bf16[18,768]{1,0:T(8,128)(2,1)S(1)}, bf16[18,768]{1,0:T(8,128)(2,1)S(1)}, u32[]{:S(2)}, u32[]{:S(2)}) collective-permute-start(bf16[18,768]{1,0:T(8,128)(2,1)S(1)} %slice.36), channel_id=1, source_target_pairs={{0,1},{1,2},{2,3},{4,5},{5,6},{6,7},{8,9},{9,10},{10,11},{12,13},{... | collective-permute-start | bytes 82952
  366.4 1.1 copy-start.9
  367.5 3.7 copy-start.8
  368.3 4.0 copy-start.33
  371.5 0.8 copy-start.18
  374.0 13.0 %all-to-all-start.1 = ((bf16[370,4,192]{0,2,1:T(8,128)(2,1)}), bf16[370,4,192]{0,2,1:T(8,128)(2,1)S(1)}, u32[]{:S(2)}, u32[]{:S(2)}) async-start(bf16[370,4,192]{0,2,1:T(8,128)(2,1)} %bitcast.133), calls=%async_computation.1 | async-start | bytes 1179648 | tf_op jit(solution)/shard_map/all_to_all | solution.py:160
  377.5 166.8 %reduce-scatter.12.cloned.1.call-start = ((), (), s32[]{:S(2)}) async-start(), calls=%async_computation.12 | async-start | bytes 2433024 | tf_op jit(solution)/shard_map/reduce_scatter | solution.py:207
  381.0 176.2 %reduce-scatter.10.cloned.1.call-start = ((), (), s32[]{:S(2)}) async-start(), calls=%async_computation.11 | async-start | bytes 2654208 | tf_op jit(solution)/shard_map/reduce_scatter | solution.py:214
  388.3 6.9 slice-start
  390.8 4.4 slice-start.1
  395.2 1.2 copy-start.15
  396.4 1.1 copy-start.13
  397.6 2.3 copy-start.5
  397.6 1.4 copy-start.7
  399.0 0.9 copy-start.4
  399.9 0.9 copy-start.2
  414.2 215.8 %reduce-scatter.14.cloned.1.call-start = ((), (), s32[]{:S(2)}) async-start(), calls=%async_computation.13 | async-start | bytes 2654208 | tf_op jit(solution)/shard_map/reduce_scatter | solution.py:216
  420.4 282.6 %reduce-scatter.16.cloned.1.call-start = ((), (), s32[]{:S(2)}) async-start(), calls=%async_computation.14 | async-start | bytes 2654208 | tf_op jit(solution)/shard_map/reduce_scatter | solution.py:218
  426.4 1.1 copy-start.6
  428.8 7.8 %copy-start.3 = (bf16[8,3,64,185]{3,2,1,0:T(8,128)(2,1)S(1)}, bf16[8,3,64,185]{3,2,1,0:T(8,128)(2,1)}, u32[]{:S(2)}) copy-start(bf16[8,3,64,185]{3,2,1,0:T(8,128)(2,1)} %copy-done.2) | copy-start | bytes 1704964
  448.2 7.6 %copy-start.28 = (f32[768]{0:T(1024)S(1)}, f32[768]{0:T(1024)}, u32[]{:S(2)}) copy-start(f32[768]{0:T(1024)} %get-tuple-element.41) | copy-start | bytes 9220
  448.2 41.0 %all-to-all-start.2 = ((bf16[1480,3,192]{2,1,0:T(4,128)(2,1)}), bf16[1480,3,192]{2,1,0:T(4,128)(2,1)}, u32[]{:S(2)}, u32[]{:S(2)}) async-start(bf16[1480,3,192]{2,1,0:T(4,128)(2,1)} %copy.75), calls=%async_computation.2 | async-start | bytes 6062080 | tf_op jit(solution)/shard_map/all_to_all | solution.py:191
  494.7 4.3 copy-start.24
  499.6 1.4 copy-start.26
  499.6 1.4 copy-start.27
Sparse Core Ops, SparseCore 0:
  59.3 23.5 all-gather.19
  85.9 55.2 all-gather.11
  142.8 22.6 all-gather.23
  167.5 23.7 all-gather.21
  193.3 41.1 all-gather.13
  236.5 39.8 all-gather.15
  277.9 29.4 all-gather.17
  384.2 100.1 reduce-scatter.11
  488.5 68.6 reduce-scatter.9
  561.1 68.8 reduce-scatter.13
  634.1 68.8 reduce-scatter.15
where the time goes:
time: 720 us; the launch traced here: 710 us
  waiting for transfers between devices  275 us (38%)
  blocking collectives  233 us (32%)
  local copies, waits for them, and re-layouts  78.2 us (11%)
  matrix products  68.1 us (9%)
  other arithmetic  21.6 us (3%)
  between operations  17.6 us (2%)
  starting transfers between devices  17.2 us (2%)
    unnamed x5, blocking collectives  176 us
    reduce_scatter x1, waiting for transfers between devices, local(): lax.psum_scatter(down_weight_part, 'dp', scatter_dimension=1, tiled=True)  73 us
    reduce_scatter x1, waiting for transfers between devices, local(): lax.psum_scatter(up_weight_part, 'dp', scatter_dimension=0, tiled=True)  72.8 us
    all_gather x1, waiting for transfers between devices, local(): lax.all_gather(up_weight, 'dp', axis=0, tiled=True)  39.5 us
    all_gather x1, blocking collectives, local(): lax.all_gather(qkv_weight, 'dp', axis=0, tiled=True)  36.1 us
    all_gather x1, waiting for transfers between devices, local(): lax.all_gather(down_weight, 'dp', axis=1, tiled=True)  35.8 us
    unnamed x111, local copies, waits for them, and re-layouts  34 us
    dot_general x4, matrix products, times_transposed(): lax.dot_general(former, latter, (((1,), (1,)), ((), ())), preferred_eleme...  23.3 us
  transfers between devices with their start and end apart: 16, of which 10 were waited for; matrix products, arithmetic and copies ran while one was open for 29% of the time, Pallas kernels for 0%

commit v1 on v0

--- a/solution.py
+++ b/solution.py
@@ -6,6 +6,21 @@
 
 HEAD_DIM = 64
 TEXT = 40
+
+
+def pack_the_case(local_block):
+    named_axis = "dp"
+    arr_out, y = (lax.axis_size(named_axis), lax.axis_index(named_axis))
+    piece_out, x_new = (local_block, 1)
+    while x_new < arr_out:
+        frame_out = lax.ppermute(
+            piece_out, axis_name=named_axis, perm=[(nth, nth ^ x_new) for nth in range(arr_out)]
+        )
+        z1 = jnp.concatenate([piece_out, frame_out], axis=1)
+        reply = jnp.concatenate([frame_out, piece_out], axis=1)
+        piece_out = jnp.where(y & x_new == 0, z1, reply)
+        x_new = 2 * x_new
+    return piece_out
 
 
 def norm_rows(values, gain, shift):
@@ -63,7 +78,7 @@
         lax.all_gather(qkv_bias, "dp", axis=1, tiled=True),
         lax.all_gather(up_weight, "dp", axis=0, tiled=True),
         lax.all_gather(up_bias, "dp", axis=0, tiled=True),
-        lax.all_gather(down_weight, "dp", axis=1, tiled=True),
+        pack_the_case(down_weight),
     )
     local_width = w_qkv.shape[2]
     heads_local = local_width // HEAD_DIM

time: 720 us -> 722 us (level)
    unnamed x111 -> x109, local copies, waits for them, and re-layouts: 34 us -> 33.9 us
  transfers between devices with their start and end apart: 16 -> 19, of which waited for: 10 -> 10; matrix products, arithmetic and copies ran while one was open for 29% -> 29% of each run, Pallas kernels for 0% -> 0%
where the time goes in v1:
time: 722 us; the launch traced here: 711 us
  waiting for transfers between devices  273 us (38%)
  blocking collectives  232 us (32%)
  local copies, waits for them, and re-layouts  78.2 us (11%)
  matrix products  71.1 us (10%)
  other arithmetic  22 us (3%)
  between operations  17.7 us (2%)
  starting transfers between devices  17.3 us (2%)
    unnamed x5, blocking collectives  176 us
    reduce_scatter x1, waiting for transfers between devices, local(): lax.psum_scatter(down_weight_part, 'dp', scatter_dimension=1, tiled=True)  73 us
    reduce_scatter x1, waiting for transfers between devices, local(): lax.psum_scatter(up_weight_part, 'dp', scatter_dimension=0, tiled=True)  72.7 us
    all_gather x1, waiting for transfers between devices, local(): lax.all_gather(up_weight, 'dp', axis=0, tiled=True)  39.9 us
    all_gather x1, blocking collectives, local(): lax.all_gather(qkv_weight, 'dp', axis=0, tiled=True)  36.1 us
    all_gather x1, waiting for transfers between devices, local(): lax.all_gather(down_weight, 'dp', axis=1, tiled=True)  35.8 us
    unnamed x109, local copies, waits for them, and re-layouts  33.9 us
    dot_general x4, matrix products, times_transposed(): lax.dot_general(former, latter, (((1,), (1,)), ((), ())), preferred_eleme...  23.3 us
  transfers between devices with their start and end apart: 19, of which 10 were waited for; matrix products, arithmetic and copies ran while one was open for 29% of the time, Pallas kernels for 0%

profile of v1, /device:TPU:0, one launch (start us, length us, event | category | flops | bytes accessed | tf_op | source)
XLA Modules:
  0.0 711.3 jit_solution(17973257282652449783)
XLA Ops:
  12.3 42.2 %all-reduce.21 = (bf16[768]{0:T(1024)(128)(2,1)S(1)}, bf16[768]{0:T(1024)(128)(2,1)S(1)}, bf16[768]{0:T(1024)(128)(2,1)S(1)}, bf16[768]{0:T(1024)(128)(2,1)S(1)}...) all-reduce(bf16[768]{0:T(1024)(128)(2,1)S(1)} %dynamic-update-slice, ...), channel_id=1, replica_groups=mesh['dp'=8,'head'=4] {'dp','head'}, use_global_device_ids=true, to_apply=%add.1 | all-reduce | flops 4608 | bytes 18432
  54.5 1.2 convert_reduce_fusion.2
  55.7 1.4 fusion.37
  57.1 2.1 fusion.46
  60.7 20.2 %all-gather.1 = bf16[8,24,2]{1,2,0:T(2,128)(2,1)S(1)} all-gather(bf16[1,24,2]{1,2,0:T(2,128)(2,1)S(1)} %bitcast.139), channel_id=1, replica_groups=mesh['dp'=8,'head'=4] {'dp'}, dimensions={0}, use_global_device_ids=true | all-gather | bytes 864 | tf_op jit(solution)/shard_map/all_gather | solution.py:78
  81.2 36.1 %all_gather.54 = bf16[768,3,192]{2,1,0:T(4,128)(2,1)S(1)} all-gather(bf16[96,3,192]{2,1,0:T(4,128)(2,1)S(1)} %copy.56), channel_id=1, replica_groups=mesh['dp'=8,'head'=4] {'dp'}, dimensions={0}, use_global_device_ids=true | all-gather | bytes 995328 | tf_op jit(solution)/shard_map/all_gather | solution.py:77
  118.4 3.8 reshape.228
  122.2 4.5 add_convert_fusion.1
  126.7 5.0 reshape.198
  131.8 1.7 fusion.60
  134.3 1.3 copy-done
  138.7 3.5 all-to-all-start
  142.3 9.4 %all-to-all-done = bf16[4,370,192]{1,2,0:T(8,128)(2,1)S(1)} async-done(((bf16[4,370,192]{1,2,0:T(8,128)(2,1)}), bf16[4,370,192]{1,2,0:T(8,128)(2,1)S(1)}, u32[]{:S(2)}, u32[]{:S(2)}) %all-to-all-start) | async-done | bytes 568352 | tf_op jit(solution)/shard_map/all_to_all | solution.py:131
  151.7 2.2 fusion.61
  156.9 5.0 collective-permute-done
  163.6 20.5 %all-reduce.5 = bf16[768]{0:T(1024)(128)(2,1)S(1)} all-reduce(bf16[768]{0:T(1024)(128)(2,1)S(1)} %dynamic-update-slice.5), channel_id=1, replica_groups=mesh['dp'=8,'head'=4] {'dp'}, use_global_device_ids=true, to_apply=%add.5 | all-reduce | flops 768 | bytes 3072
  184.5 3.6 reshape.225
  188.1 3.2 all-gather.22.cloned.1.call-done
  191.3 3.6 reshape.223
  194.9 39.9 %all-gather.14.cloned.1.call-done = bf16[768,768]{1,0:T(8,128)(2,1)} async-done(((bf16[96,768]{1,0:T(8,128)(2,1)}), bf16[768,768]{1,0:T(8,128)(2,1)}) %all-gather.14.cloned.1.call-update) | async-done | bytes 1179664 | tf_op jit(solution)/shard_map/all_gather | solution.py:79
  234.8 6.1 fusion.62
  240.9 35.8 %all-gather.16.cloned.1.call-done = bf16[768,768]{0,1:T(8,128)(2,1)} async-done(((bf16[768,96]{0,1:T(8,128)(2,1)}), bf16[768,768]{0,1:T(8,128)(2,1)}) %all-gather.16.cloned.1.call-update) | async-done | bytes 1179664 | tf_op jit(solution)/shard_map/all_gather | solution.py:154
  276.7 14.9 %convert_reduce_fusion = (f32[768]{0:T(1024)}, bf16[1480,768]{1,0:T(8,128)(2,1)S(1)}, f32[1480,768]{1,0:T(8,128)S(1)}) fusion(f32[1480,768]{1,0:T(8,128)} %fusion.62, f32[768]{0:T(1024)S(1)} %convert_element_type.133, bf16[1480,768]{1,0:T(8,128)(2,1)} %reshape.225, bf16[768,768]{0,1:T(8,128)(2,1)} %all-gather.16.cloned.1.call-done), kind=kOutput, calls=%fused_computation.8 | convolution fusion | flops 1831126272 | bytes 14825472 | tf_op jit(solution)/shard_map/dot_general | solution.py:40
  293.7 3.5 convolution_convert_fusion
  297.2 4.7 convolution_convert_fusion.1
  301.9 54.1 %fusion.53 = (bf16[376,768]{1,0:T(8,128)(2,1)S(1)}, bf16[376,768]{1,0:T(8,128)(2,1)S(1)}) fusion(bf16[1480,768]{1,0:T(8,128)(2,1)} %convolution_convert_fusion.1, bf16[1480,768]{1,0:T(8,128)(2,1)} %convolution_convert_fusion), kind=kCustom, calls=%all-reduce-scatter.2 | all-reduce-scatter fusion | flops 2310145 | bytes 5702144
  356.0 1.3 collective-permute-start.3
  357.4 3.2 collective-permute-start.4
  362.5 4.2 concatenate.29
  366.6 1.3 concatenate.30
  367.9 1.1 fusion.39
  369.9 3.0 fusion.56
  375.6 3.5 all-to-all-start.1
  379.2 3.5 fusion.64
  382.7 5.9 all-to-all-done.1
  388.6 1.3 copy.66
  389.9 2.5 reshape.199
  392.5 4.5 multiply_reduce_fusion
  397.1 1.2 multiply_convert_fusion
  402.6 2.8 copy.78
  405.5 4.9 reshape.202
  410.4 5.6 fusion.63
  416.3 5.9 fusion.65
  422.3 5.9 fusion.66
  428.2 1.1 copy-done.6
  429.3 1.3 copy.69
  430.7 2.7 stack.33
  433.4 2.5 copy.71
  435.8 2.6 stack.34
  438.5 1.3 copy.74
  439.8 2.0 stack.35
  441.8 2.7 pad_maximum_fusion.1
  444.5 5.5 copy.75
  450.0 4.8 all-to-all-start.2
  456.1 1.5 convert_reduce_fusion.5
  457.6 19.7 %all-reduce.20 = (f32[2,192]{1,0:T(2,128)S(1)}, f32[768]{0:T(1024)S(1)}) all-reduce(f32[2,192]{1,0:T(2,128)S(1)} %pad_maximum_fusion.2, f32[768]{0:T(1024)S(1)} %copy-done.28), channel_id=7, replica_groups=mesh['dp'=8,'head'=4] {'dp'}, use_global_device_ids=true, to_apply=%region_20.21.clone | all-reduce | flops 1152 | bytes 9216
  478.5 12.5 %all-to-all-done.2 = bf16[1480,3,192]{2,1,0:T(4,128)(2,1)} async-done(((bf16[1480,3,192]{2,1,0:T(4,128)(2,1)}), bf16[1480,3,192]{2,1,0:T(4,128)(2,1)}, u32[]{:S(2)}, u32[]{:S(2)}) %all-to-all-start.2) | async-done | bytes 1704992 | tf_op jit(solution)/shard_map/all_to_all | solution.py:206
  491.0 5.6 copy.76
  496.6 4.2 fusion.52
  501.6 1.4 convert_reduce_fusion.3
  503.0 39.5 %all-reduce.19 = (f32[768]{0:T(1024)S(1)}, f32[768]{0:T(1024)S(1)}, f32[768]{0:T(1024)S(1)}, f32[768]{0:T(1024)S(1)}, f32[768]{0:T(1024)S(1)}, /*index=5*/f32[768]{0:T(1024)S(1)}) all-reduce(f32[768]{0:T(1024)S(1)} %get-tuple-element.18, f32[768]{0:T(1024)S(1)} %get-tuple-element.20, ...), channel_id=4, replica_groups=mesh['dp'=8,'head'=4] {'dp','head'}, use_global_device_ids=true, to_apply=%region_14.15.clone | all-reduce | flops 4608 | bytes 36864
  545.9 12.7 %reduce-scatter.10.cloned.1.call-done = f32[96,3,192]{2,0,1:T(8,128)} async-done(((f32[768,3,192]{2,0,1:T(8,128)}), f32[96,3,192]{2,0,1:T(8,128)}) %reduce-scatter.10.cloned.1.call-update) | async-done | bytes 221200 | tf_op jit(solution)/shard_map/reduce_scatter | solution.py:229
  558.6 72.7 %reduce-scatter.14.cloned.1.call-done = f32[96,768]{1,0:T(8,128)} async-done(((f32[768,768]{1,0:T(8,128)}), f32[96,768]{1,0:T(8,128)}) %reduce-scatter.14.cloned.1.call-update) | async-done | bytes 294928 | tf_op jit(solution)/shard_map/reduce_scatter | solution.py:231
  631.4 73.0 %reduce-scatter.16.cloned.1.call-done = f32[768,96]{0,1:T(8,128)} async-done(((f32[768,768]{0,1:T(8,128)}), f32[768,96]{0,1:T(8,128)}) %reduce-scatter.16.cloned.1.call-update) | async-done | bytes 294928 | tf_op jit(solution)/shard_map/reduce_scatter | solution.py:233
  (180 shorter events, 33.2 us)
Async XLA Ops:
  7.2 53.6 %copy-start.30 = (bf16[2,24]{1,0:T(2,128)(2,1)S(1)}, bf16[2,24]{1,0:T(2,128)(2,1)}, u32[]{:S(2)}) copy-start(bf16[2,24]{1,0:T(2,128)(2,1)} %param.20) | copy-start | bytes 292
  7.2 73.8 %copy-start.22 = (bf16[96,3,192]{2,0,1:T(8,128)(2,1)S(1)}, bf16[96,3,192]{2,0,1:T(8,128)(2,1)}, u32[]{:S(2)}) copy-start(bf16[96,3,192]{2,0,1:T(8,128)(2,1)} %param.19) | copy-start | bytes 331780
  7.2 111.2 %all-gather.20.cloned.1.call-start = ((), (), s32[]{:S(2)}) async-start(), calls=%async_computation.15 | async-start | bytes 2887680 | tf_op jit(solution)/shard_map/all_gather | solution.py:91
  57.0 61.1 %copy-start.23 = (f32[370]{0:T(512)}, f32[370]{0:T(512)S(1)}, u32[]{:S(2)}) copy-start(f32[370]{0:T(512)S(1)} %fusion.37) | copy-start | bytes 4444
  59.2 83.1 %all-gather.12.cloned.1.call-start = ((), (), s32[]{:S(2)}) async-start(), calls=%async_computation.7 | async-start | bytes 1216512 | tf_op jit(solution)/shard_map/all_gather | solution.py:70
  60.0 124.5 %all-gather.24.cloned.1.call-start = ((), (), s32[]{:S(2)}) async-start(), calls=%async_computation.17 | async-start | bytes 2887680 | tf_op jit(solution)/shard_map/all_gather | solution.py:160
  81.0 37.3 %copy-start.32 = (s32[8]{0:T(128)S(1)}, s32[8]{0:T(128)}, u32[]{:S(2)}) copy-start(s32[8]{0:T(128)} %param.16) | copy-start | bytes 100
  118.2 4.0 copy-start.11
  131.8 1.7 copy-start.12
  131.8 1.7 copy-start.14
  131.8 2.5 copy-start.16
  133.5 2.1 copy-start
  137.1 14.6 %copy-start.1 = (bf16[370,768]{1,0:T(8,128)(2,1)S(1)}, bf16[370,768]{1,0:T(8,128)(2,1)}, u32[]{:S(2)}) copy-start(bf16[370,768]{1,0:T(8,128)(2,1)} %param.15) | copy-start | bytes 1704964
  138.7 13.0 %all-to-all-start = ((bf16[4,370,192]{1,2,0:T(8,128)(2,1)}), bf16[4,370,192]{1,2,0:T(8,128)(2,1)S(1)}, u32[]{:S(2)}, u32[]{:S(2)}) async-start(bf16[4,370,192]{1,2,0:T(8,128)(2,1)} %copy.64), calls=%async_computation | async-start | bytes 1179648 | tf_op jit(solution)/shard_map/all_to_all | solution.py:131
  142.2 49.1 %all-gather.22.cloned.1.call-start = ((), (), s32[]{:S(2)}) async-start(), calls=%async_computation.16 | async-start | bytes 2887680 | tf_op jit(solution)/shard_map/all_gather | solution.py:139
  151.7 2.5 copy-start.17
  154.0 2.6 copy-start.21
  154.3 29.9 %copy-start.25 = (f32[370]{0:T(512)}, f32[370]{0:T(512)S(1)}, u32[]{:S(2)}) copy-start(f32[370]{0:T(512)S(1)} %multiply_reduce_fusion.1) | copy-start | bytes 4444
  154.3 7.8 %copy-start.29 = (u32[32]{0:T(128)S(1)}, u32[32]{0:T(128)}, u32[]{:S(2)}) copy-start(u32[32]{0:T(128)} %constant.134) | copy-start | bytes 388
  154.3 9.1 %copy-start.35 = (bf16[96]{0:T(256)(128)(2,1)S(1)}, bf16[96]{0:T(256)(128)(2,1)}, u32[]{:S(2)}) copy-start(bf16[96]{0:T(256)(128)(2,1)} %param.26) | copy-start | bytes 580
  155.4 79.4 %all-gather.14.cloned.1.call-start = ((), (), s32[]{:S(2)}) async-start(), calls=%async_computation.8 | async-start | bytes 1327104 | tf_op jit(solution)/shard_map/all_gather | solution.py:79
  156.0 120.7 %all-gather.16.cloned.1.call-start = ((), (), s32[]{:S(2)}) async-start(), calls=%async_computation.9 | async-start | bytes 1327104 | tf_op jit(solution)/shard_map/all_gather | solution.py:154
  156.6 340.0 %all-gather.18.cloned.1.call-start = ((), (), s32[]{:S(2)}) async-start(), calls=%async_computation.10 | async-start | bytes 4423680 | tf_op jit(solution)/shard_map/all_gather | solution.py:213
  156.6 5.3 collective-permute-start
  162.0 22.2 %collective-permute-start.1 = (bf16[768,192]{0,1:T(8,128)(2,1)S(1)}, bf16[768,192]{0,1:T(8,128)(2,1)S(1)}, u32[]{:S(2)}, u32[]{:S(2)}) collective-permute-start(bf16[768,192]{0,1:T(8,128)(2,1)S(1)} %maximum_select_fusion.3), channel_id=1, source_target_pairs={{0,8},{4,12},{8,0},{12,4},{16,24},{20,28},{24,16},{28,20},{1,9},{5... | collective-permute-start | bytes 884744 | tf_op jit(solution)/shard_map/ppermute | solution.py:16
  184.4 112.8 %collective-permute-start.2 = (bf16[768,384]{0,1:T(8,128)(2,1)S(1)}, bf16[768,384]{0,1:T(8,128)(2,1)}, u32[]{:S(2)}, u32[]{:S(2)}) collective-permute-start(bf16[768,384]{0,1:T(8,128)(2,1)S(1)} %maximum_select_fusion.2), channel_id=1, source_target_pairs={{0,16},{4,20},{8,24},{12,28},{16,0},{20,4},{24,8},{28,12},{1,17},{... | collective-permute-start | bytes 1769480 | tf_op jit(solution)/shard_map/ppermute | solution.py:16
  276.7 14.9 %copy-start.10 = (f32[1480,768]{1,0:T(8,128)S(1)}, f32[1480,768]{1,0:T(8,128)}, u32[]{:S(2)}) copy-start(f32[1480,768]{1,0:T(8,128)} %fusion.62) | copy-start | bytes 13639684
  291.6 1.4 copy-start.20
  291.6 2.1 copy-start.34
  292.5 4.7 copy-start.19
  301.9 58.7 %copy-start.31 = (u32[32]{0:T(128)S(1)}, u32[32]{0:T(128)}, u32[]{:S(2)}) copy-start(u32[32]{0:T(128)} %constant.144) | copy-start | bytes 388
  356.0 6.4 collective-permute-start.3
  357.4 9.3 %collective-permute-start.4 = (bf16[18,768]{1,0:T(8,128)(2,1)S(1)}, bf16[18,768]{1,0:T(8,128)(2,1)S(1)}, u32[]{:S(2)}, u32[]{:S(2)}) collective-permute-start(bf16[18,768]{1,0:T(8,128)(2,1)S(1)} %slice.36), channel_id=1, source_target_pairs={{0,1},{1,2},{2,3},{4,5},{5,6},{6,7},{8,9},{9,10},{10,11},{12,13},{... | collective-permute-start | bytes 82952
  367.9 1.2 copy-start.9
  369.1 3.7 copy-start.8
  369.9 4.1 copy-start.33
  373.1 0.8 copy-start.18
  375.6 13.0 %all-to-all-start.1 = ((bf16[370,4,192]{0,2,1:T(8,128)(2,1)}), bf16[370,4,192]{0,2,1:T(8,128)(2,1)S(1)}, u32[]{:S(2)}, u32[]{:S(2)}) async-start(bf16[370,4,192]{0,2,1:T(8,128)(2,1)} %bitcast.132), calls=%async_computation.1 | async-start | bytes 1179648 | tf_op jit(solution)/shard_map/all_to_all | solution.py:175
  379.1 166.8 %reduce-scatter.12.cloned.1.call-start = ((), (), s32[]{:S(2)}) async-start(), calls=%async_computation.12 | async-start | bytes 2433024 | tf_op jit(solution)/shard_map/reduce_scatter | solution.py:222
  382.7 176.0 %reduce-scatter.10.cloned.1.call-start = ((), (), s32[]{:S(2)}) async-start(), calls=%async_computation.11 | async-start | bytes 2654208 | tf_op jit(solution)/shard_map/reduce_scatter | solution.py:229
  389.9 7.1 slice-start
  392.5 4.6 slice-start.1
  397.0 1.3 copy-start.15
  398.3 1.1 copy-start.13
  399.4 2.3 copy-start.5
  399.5 1.4 copy-start.7
  400.9 0.9 copy-start.4
  401.8 0.9 copy-start.2
  416.1 215.3 %reduce-scatter.14.cloned.1.call-start = ((), (), s32[]{:S(2)}) async-start(), calls=%async_computation.13 | async-start | bytes 2654208 | tf_op jit(solution)/shard_map/reduce_scatter | solution.py:231
  422.2 282.1 %reduce-scatter.16.cloned.1.call-start = ((), (), s32[]{:S(2)}) async-start(), calls=%async_computation.14 | async-start | bytes 2654208 | tf_op jit(solution)/shard_map/reduce_scatter | solution.py:233
  428.2 1.1 copy-start.6
  430.7 7.8 %copy-start.3 = (bf16[8,3,64,185]{3,2,1,0:T(8,128)(2,1)S(1)}, bf16[8,3,64,185]{3,2,1,0:T(8,128)(2,1)}, u32[]{:S(2)}) copy-start(bf16[8,3,64,185]{3,2,1,0:T(8,128)(2,1)} %copy-done.2) | copy-start | bytes 1704964
  450.0 7.6 %copy-start.28 = (f32[768]{0:T(1024)S(1)}, f32[768]{0:T(1024)}, u32[]{:S(2)}) copy-start(f32[768]{0:T(1024)} %get-tuple-element.41) | copy-start | bytes 9220
  450.0 41.0 %all-to-all-start.2 = ((bf16[1480,3,192]{2,1,0:T(4,128)(2,1)}), bf16[1480,3,192]{2,1,0:T(4,128)(2,1)}, u32[]{:S(2)}, u32[]{:S(2)}) async-start(bf16[1480,3,192]{2,1,0:T(4,128)(2,1)} %copy.75), calls=%async_computation.2 | async-start | bytes 6062080 | tf_op jit(solution)/shard_map/all_to_all | solution.py:206
  496.6 4.2 copy-start.24
  501.5 1.4 copy-start.26
  501.5 1.4 copy-start.27
Sparse Core Ops, SparseCore 0:
  59.4 23.5 all-gather.19
  85.9 55.2 all-gather.11
  142.8 22.7 all-gather.23
  167.6 23.6 all-gather.21
  193.3 41.4 all-gather.13
  236.8 39.8 all-gather.15
  278.2 29.4 all-gather.17
  385.8 100.0 reduce-scatter.11
  489.9 68.6 reduce-scatter.9
  562.5 68.7 reduce-scatter.13
  635.4 68.8 reduce-scatter.15
